TPU v7x, 32 devices: a whole 2x2x4 slice. The times are simulated.
32 devices in a mesh: aa: 8 (over z, y), ba: 4 (over x, core).
Axes of the slice: x: 2, y: 2, z: 4, core: 2. Of those that a mesh axis runs over, the one named last changes fastest.
Arguments:
- features: bfloat16 [65536, 256], P(('aa', 'ba')), may hold values from -6 to 6
- tile_ids: int32 [65536, 1], P(('aa', 'ba')), may hold values from 0 to 31; in each aligned block of 2048 rows (0 to 2047, 2048 to 4095, ...) at most 96 rows name the same one
- cell_ids: int32 [65536], P(('aa', 'ba')), may hold values from 0 to 8191
- spread_weight: float32 [65536], P(('aa', 'ba')), may hold values from 0.1 to 0.6
- read_weight: float32 [65536], P(('aa', 'ba')), may hold values from 0.5 to 2
- message_weight: bfloat16 [256, 256], replicated, may hold values from -0.375 to 0.375
- skip_weight: bfloat16 [256, 256], replicated, may hold values from -0.375 to 0.375
- spectral_weight: bfloat16 [16, 256, 256, 256], P('ba', 'aa'), may hold values from -1.5 to 1.5
- hidden_weight: bfloat16 [256, 256], replicated, may hold values from -0.375 to 0.375
- output_weight: bfloat16 [256, 256], replicated, may hold values from -0.75 to 0.75
Outputs:
- point_out: bfloat16 [65536, 256], P(('aa', 'ba'))
Inputs may be any that keep to these rules, and one draw needn't show every extreme that they name: `tile_ids`: among the rows of one device no index appears more than 96 times, and some index appears exactly 96 times.
All inputs are finite; a program needn't handle non-finite values.
Results may differ from a plain program's by a relative error of at most 0.015.
Values may be sent and summed in bfloat16 or wider, within the bound.
A program may use at most 64 MiB of HBM per device.

v0:
```python
import functools
import math

import jax
import jax.numpy as jnp
import numpy as np
from jax import lax
from jax.experimental import pallas as pl
from jax.experimental.pallas import tpu as pltpu
from jax.sharding import PartitionSpec as P

G = 64
F32 = jnp.float32
BF16 = jnp.bfloat16


def basis_np(modes, grid):
    k = np.arange(modes)[:, None]
    half = modes // 2
    freq = np.where(k < half, k, k - half + 1).astype(np.float64)
    phase = 2.0 * math.pi * freq * np.arange(grid)[None, :] / grid
    wave = np.where(k < half, np.cos(phase), np.sin(phase))
    norm = np.where(k == 0, math.sqrt(1.0 / grid), math.sqrt(2.0 / grid))
    return (wave * norm).astype(np.float32)


def split_table(table):
    high = table.astype(BF16)
    low = (table - high.astype(np.float32)).astype(BF16)
    return np.concatenate([high, low], axis=0)


def dot(a, b):
    return jnp.dot(a, b, preferred_element_type=F32)


def blocks_of(rows, want):
    return want if rows % want == 0 else rows


def pack_kernel(devices, capacity, tiles_ref, cells_ref, message_ref, rows_ref, where_ref, slots_ref, slots):
    block = rows_ref.shape[0]
    points = message_ref.shape[0]

    @pl.when(pl.program_id(0) == 0)
    def _():
        step = blocks_of(points, 256)
        upper = (
            lax.broadcasted_iota(jnp.int32, (step, step), 0)
            <= lax.broadcasted_iota(jnp.int32, (step, step), 1)
        ).astype(F32).astype(BF16)
        carry = jnp.zeros((devices, 1), F32)
        for start in range(0, points, step):
            tiles = tiles_ref[:, start : start + step]
            hot = (lax.broadcasted_iota(jnp.int32, (devices, step), 0) == tiles).astype(F32)
            counts = dot(hot.astype(BF16), upper) + carry
            rank = jnp.sum(counts * hot, axis=0, keepdims=True) - 1.0
            slots[:, start : start + step] = tiles * capacity + rank.astype(jnp.int32)
            carry = carry + jnp.sum(hot, axis=1, keepdims=True)
        slots_ref[...] = slots[...]

    own = lax.broadcasted_iota(jnp.int32, (block, points), 0) + pl.program_id(0) * block
    hot = (own == slots[...]).astype(F32).astype(BF16)
    rows_ref[...] = dot(hot, message_ref[...]).astype(BF16)
    found = dot(hot, cells_ref[...])
    where_ref[...] = found[:, 0:1] * G + found[:, 1:2] + (found[:, 2:3] - 1.0)


def pack(tiles, cells, message, devices, capacity):
    points, width = message.shape
    total = devices * capacity
    block = blocks_of(total, 256)
    return pl.pallas_call(
        functools.partial(pack_kernel, devices, capacity),
        grid=(total // block,),
        in_specs=[
            pl.BlockSpec((1, points), lambda i: (0, 0)),
            pl.BlockSpec(cells.shape, lambda i: (0, 0)),
            pl.BlockSpec((points, width), lambda i: (0, 0)),
        ],
        out_specs=[
            pl.BlockSpec((block, width), lambda i: (i, 0)),
            pl.BlockSpec((block, 1), lambda i: (i, 0)),
            pl.BlockSpec((1, points), lambda i: (0, 0)),
        ],
        out_shape=[
            jax.ShapeDtypeStruct((total, width), BF16),
            jax.ShapeDtypeStruct((total, 1), F32),
            jax.ShapeDtypeStruct((1, points), jnp.int32),
        ],
        scratch_shapes=[pltpu.VMEM((1, points), jnp.int32)],
        cost_estimate=pl.CostEstimate(
            flops=4 * total * points * width, bytes_accessed=6 * total * width, transcendentals=0
        ),
        name="pack",
    )(tiles, cells, message)


def merge_kernel(column_ref, row_ref, rows_ref, out_ref):
    same = (column_ref[...] == row_ref[...]).astype(F32).astype(BF16)
    out_ref[...] = dot(same, rows_ref[...]).astype(BF16)


def merge(where, rows):
    total, width = rows.shape
    block = blocks_of(total, 256)
    return pl.pallas_call(
        merge_kernel,
        grid=(total // block,),
        in_specs=[
            pl.BlockSpec((block, 1), lambda i: (i, 0)),
            pl.BlockSpec((1, total), lambda i: (0, 0)),
            pl.BlockSpec((total, width), lambda i: (0, 0)),
        ],
        out_specs=pl.BlockSpec((block, width), lambda i: (i, 0)),
        out_shape=jax.ShapeDtypeStruct((total, width), BF16),
        cost_estimate=pl.CostEstimate(
            flops=2 * total * total * width, bytes_accessed=4 * total * width, transcendentals=0
        ),
        name="merge",
    )(where.reshape(total, 1), where.reshape(1, total), rows)


def hot_rows(values, points):
    lane = lax.broadcasted_iota(jnp.int32, (2 * G, points), 0) % G
    return (lane == values).astype(F32).astype(BF16)


def hot_columns(values, points):
    lane = lax.broadcasted_iota(jnp.int32, (points, 2 * G), 1) % G
    return (lane == values).astype(F32).astype(BF16)


def forward_kernel(x_ref, y_ref, z_ref, tx_ref, ty_ref, tz_ref, message_ref, out_ref, plane, second):
    points = message_ref.shape[0]
    j = pl.program_id(0)

    @pl.when(j == 0)
    def _():
        plane[...] = dot(tx_ref[...], hot_rows(x_ref[...], points)) * dot(
            tz_ref[...], hot_rows(z_ref[...], points)
        )
        second[...] = dot(ty_ref[...], hot_rows(y_ref[...], points))

    scaled = (plane[...] * second[pl.ds(j, 1), :]).astype(BF16)
    result = dot(scaled, message_ref[...])
    out_ref[...] = result.reshape(out_ref.shape).astype(BF16)


def forward(x, y, z, tables, message, axis_first, modes):
    points, width = message.shape
    tx, ty, tz = tables
    pairs = tx.shape[1]
    share = pairs // axis_first
    whole = lambda shape: pl.BlockSpec(shape, lambda j: (0,) * len(shape))
    return pl.pallas_call(
        forward_kernel,
        grid=(modes,),
        in_specs=[whole((1, points))] * 3
        + [whole((pairs, 2 * G)), whole((modes, 2 * G)), whole((pairs, 2 * G)), whole((points, width))],
        out_specs=pl.BlockSpec((axis_first, 1, share, width), lambda j: (0, j, 0, 0)),
        out_shape=jax.ShapeDtypeStruct((axis_first, modes, share, width), BF16),
        scratch_shapes=[pltpu.VMEM((pairs, points), F32), pltpu.VMEM((modes, points), F32)],
        cost_estimate=pl.CostEstimate(
            flops=2 * modes * pairs * points * width,
            bytes_accessed=2 * modes * pairs * width,
            transcendentals=0,
        ),
        name="forward",
    )(x, y, z, tx.T, ty.T, tz.T, message)


def inverse_kernel(modes, x_ref, y_ref, z_ref, tx_ref, ty_ref, tz_ref, mixed_ref, out_ref):
    points, width = out_ref.shape
    pairs = tx_ref.shape[1]
    plane = dot(hot_columns(x_ref[...], points), tx_ref[...]) * dot(
        hot_columns(z_ref[...], points), tz_ref[...]
    )
    second = dot(hot_columns(y_ref[...], points), ty_ref[...])
    total = jnp.zeros((points, width), F32)
    for j in range(modes):
        part = mixed_ref[:, j]
        if part.shape[1] % 16:
            part = part.astype(F32)
        part = part.reshape(pairs, width).astype(BF16)
        total = total + dot((plane * second[:, j : j + 1]).astype(BF16), part)
    out_ref[...] = total


def inverse(x, y, z, tables, mixed):
    points = x.shape[0]
    tx, ty, tz = tables
    modes, width = mixed.shape[1], mixed.shape[3]
    pairs = tx.shape[1]
    block = blocks_of(points, 256)
    whole = lambda shape: pl.BlockSpec(shape, lambda i: (0,) * len(shape))
    column = pl.BlockSpec((block, 1), lambda i: (i, 0))
    return pl.pallas_call(
        functools.partial(inverse_kernel, modes),
        grid=(points // block,),
        in_specs=[column] * 3 + [whole(tx.shape), whole(ty.shape), whole(tz.shape), whole(mixed.shape)],
        out_specs=pl.BlockSpec((block, width), lambda i: (i, 0)),
        out_shape=jax.ShapeDtypeStruct((points, width), F32),
        cost_estimate=pl.CostEstimate(
            flops=2 * modes * pairs * points * width,
            bytes_accessed=2 * modes * pairs * width,
            transcendentals=0,
        ),
        name="inverse",
    )(x, y, z, tx, ty, tz, mixed)


def decode_kernel(slots_ref, returned_ref, inverse_ref, read_ref, skip_ref, hidden_ref, output_ref, out_ref):
    block = out_ref.shape[0]
    total = returned_ref.shape[0]
    lane = lax.broadcasted_iota(jnp.int32, (block, total), 1)
    hot = (lane == slots_ref[...]).astype(F32).astype(BF16)
    latent = dot(hot, returned_ref[...]).astype(BF16)
    latent_out = jax.nn.gelu(inverse_ref[...] + dot(latent, skip_ref[...])).astype(BF16)
    gathered = (read_ref[...] * latent_out.astype(F32)).astype(BF16)
    hidden = jax.nn.gelu(dot(gathered, hidden_ref[...])).astype(BF16)
    out_ref[...] = dot(hidden, output_ref[...]).astype(BF16)


def decode(slots, returned, inverse_values, read, skip_weight, hidden_weight, output_weight):
    points, width = inverse_values.shape
    total = returned.shape[0]
    block = blocks_of(points, 256)
    whole = lambda shape: pl.BlockSpec(shape, lambda i: (0,) * len(shape))
    column = pl.BlockSpec((block, 1), lambda i: (i, 0))
    rows = pl.BlockSpec((block, width), lambda i: (i, 0))
    return pl.pallas_call(
        decode_kernel,
        grid=(points // block,),
        in_specs=[column, whole((total, width)), rows, column] + [whole((width, width))] * 3,
        out_specs=rows,
        out_shape=jax.ShapeDtypeStruct((points, width), BF16),
        cost_estimate=pl.CostEstimate(
            flops=2 * points * total * width, bytes_accessed=4 * total * width, transcendentals=0
        ),
        name="decode",
    )(slots, returned, inverse_values, read, skip_weight, hidden_weight, output_weight)


def per_device(
    features,
    tile_ids,
    cell_ids,
    spread_weight,
    read_weight,
    message_weight,
    skip_weight,
    spectral_weight,
    hidden_weight,
    output_weight,
):
    axes = ("aa", "ba")
    points, width = features.shape
    axis_first = lax.axis_size("aa")
    axis_second = lax.axis_size("ba")
    devices = axis_first * axis_second
    capacity = 3 * points // (2 * devices)
    tile_x = G // axis_first
    tile_y = G // axis_second
    modes_y, share = spectral_weight.shape[0], spectral_weight.shape[1]
    modes = modes_y * axis_second

    basis = basis_np(modes, G)
    tx = split_table(np.repeat(basis, modes, axis=0).T)
    tz = split_table(np.tile(basis, (modes, 1)).T)
    ty = split_table(basis.T)
    tables = (jnp.asarray(tx), jnp.asarray(ty), jnp.asarray(tz))

    targets = tile_ids[:, 0]
    x = targets // axis_second * tile_x + cell_ids // (tile_y * G)
    y = targets % axis_second * tile_y + cell_ids // G % tile_y
    z = cell_ids % G

    product = dot(features, message_weight)
    message = (spread_weight[:, None] * product).astype(BF16)
    marks = jnp.stack([cell_ids // G, cell_ids % G, jnp.ones_like(cell_ids)], axis=1)
    marks = jnp.pad(marks.astype(BF16), ((0, 0), (0, 125)))
    send_rows, send_where, slots = pack(targets[None, :], marks, message, devices, capacity)
    recv_where = lax.all_to_all(
        send_where.reshape(devices, capacity), axes, split_axis=0, concat_axis=0, tiled=True
    )
    recv_rows = lax.all_to_all(send_rows, axes, split_axis=0, concat_axis=0, tiled=True)

    partial = forward(x[None, :], y[None, :], z[None, :], tables, message, axis_first, modes)
    partial = partial.reshape(devices, modes_y, share, width)
    spectrum = lax.psum_scatter(partial, axes, scatter_dimension=0, tiled=True)[0]
    mixed = jnp.einsum(
        "jmc,jmco->jmo", spectrum, spectral_weight, preferred_element_type=F32
    ).astype(BF16)
    gathered = lax.all_gather(mixed, axes, axis=0)
    gathered = gathered.reshape(axis_first, modes, share, width)

    merged = merge(recv_where, recv_rows)
    returned = lax.all_to_all(merged, axes, split_axis=0, concat_axis=0, tiled=True)
    values = inverse(x[:, None], y[:, None], z[:, None], tables, gathered)
    return decode(
        slots.reshape(points, 1), returned, values, read_weight[:, None],
        skip_weight, hidden_weight, output_weight,
    )


def solution(mesh):
    placed = (
        P(("aa", "ba"), None),
        P(("aa", "ba"), None),
        P(("aa", "ba")),
        P(("aa", "ba")),
        P(("aa", "ba")),
        P(),
        P(),
        P("ba", "aa", None, None),
        P(),
        P(),
    )
    return jax.shard_map(
        per_device, mesh=mesh, in_specs=placed, out_specs=P(("aa", "ba"), None), check_vma=False
    )
```

profile of v0, /device:TPU:0, one launch (start us, length us, event | category | flops | bytes accessed | tf_op | source)
XLA Modules:
  0.0 267.7 jit_solution(18222409728918219470)
XLA Ops:
  6.5 1.4 fusion.7
  8.0 2.3 fusion.message_ref
  10.3 11.5 %forward.1 = bf16[8,16,32,256]{3,2,1,0:T(8,128)(2,1)} custom-call(s32[1,2048]{1,0:T(1,128)} %bitcast.41, s32[1,2048]{1,0:T(1,128)} %bitcast.39, s32[1,2048]{1,0:T(1,128)} %bitcast.35, bf16[256,128]{1,0:T(8,128)(2,1)} %constant.95.tx_ref, bf16[16,128]{1,0:T(8,128)(2,1)} %constant.96.ty_ref, bf16[256,128]{1,0:T(8,128)(2,1)} %constant.97.tz_ref, ...), custom_call_target="tpu_custom_call" | custom-call | flops 4294967296 | bytes 2097152 | tf_op jit(solution)/shard_map/forward/pallas_call | solution.py:156
  23.0 0.9 pad.4.cells_ref
  23.9 11.8 %pack.1 = (bf16[3072,256]{1,0:T(8,128)(2,1)}, f32[3072,1]{1,0:T(8,128)}, s32[1,2048]{1,0:T(1,128)}) custom-call(s32[1,2048]{1,0:T(1,128)} %bitcast.46, bf16[2048,128]{1,0:T(8,128)(2,1)} %pad.4.cells_ref, bf16[2048,256]{1,0:T(8,128)(2,1)} %fusion.message_ref), custom_call_target="tpu_custom_call" | custom-call | flops 6442450944 | bytes 4718592 | tf_op jit(solution)/shard_map/pack/pallas_call | solution.py:73
  35.7 1.9 reduce
  37.7 14.3 %all_to_all.31 = f32[32,1,96]{2,1,0:T(1,128)S(1)} all-to-all(f32[32,1,96]{2,1,0:T(1,128)S(1)} %bitcast.38), channel_id=1, replica_groups=mesh['aa'=8,'ba'=4] {'aa','ba'}, dimensions={0} | all-to-all | bytes 24576 | tf_op jit(solution)/shard_map/all_to_all | solution.py:284
  52.0 2.7 %all-to-all-start.1 = ((bf16[32,96,256]{2,1,0:T(8,128)(2,1)}), bf16[32,96,256]{2,1,0:T(8,128)(2,1)S(1)}, u32[]{:S(2)}, u32[]{:S(2)}) async-start(bf16[32,96,256]{2,1,0:T(8,128)(2,1)} %bitcast.28), calls=%async_computation.1 | async-start | bytes 3145728 | tf_op jit(solution)/shard_map/all_to_all | solution.py:287
  54.7 109.8 %reduce-scatter.2.cloned.1.call-done = bf16[1,4,32,256]{3,2,1,0:T(8,128)(2,1)} async-done(((bf16[32,4,32,256]{3,2,1,0:T(8,128)(2,1)}), bf16[1,4,32,256]{3,2,1,0:T(8,128)(2,1)}) %reduce-scatter.2.cloned.1.call-update) | async-done | bytes 65552 | tf_op jit(solution)/shard_map/reduce_scatter | solution.py:291
  164.5 8.1 %fusion.1 = bf16[4,32,1,256]{3,2,1,0:T(2,128)(2,1)S(1)} fusion(bf16[4,32,256,256]{3,2,1,0:T(8,128)(2,1)} %param.20, bf16[4,32,256,1]{2,1,0,3:T(8,128)(2,1)} %bitcast.32), kind=kOutput, calls=%fused_computation.3 | convolution fusion | flops 16777216 | bytes 16908288 | tf_op jit(solution)/shard_map/jmc,jmco->jmo/dot_general | solution.py:292
  173.8 0.7 reduce.6
  174.5 2.6 reshape.35.column_ref
  177.8 1.2 copy-done.1
  179.0 11.4 %merge.1 = bf16[3072,256]{1,0:T(8,128)(2,1)} custom-call(f32[3072,1]{1,0:T(8,128)} %reshape.35.column_ref, f32[1,3072]{1,0:T(1,128)} %reshape.28.row_ref, bf16[3072,256]{1,0:T(8,128)(2,1)} %bitcast.29), custom_call_target="tpu_custom_call" | custom-call | flops 4831838208 | bytes 3145728 | tf_op jit(solution)/shard_map/merge/pallas_call | solution.py:107
  190.4 2.8 %all-to-all-start.2 = ((bf16[32,96,256]{2,1,0:T(8,128)(2,1)}), bf16[32,96,256]{2,1,0:T(8,128)(2,1)S(1)}, u32[]{:S(2)}, u32[]{:S(2)}) async-start(bf16[32,96,256]{2,1,0:T(8,128)(2,1)} %bitcast.31), calls=%async_computation.2 | async-start | bytes 3145728 | tf_op jit(solution)/shard_map/all_to_all | solution.py:299
  193.2 1.4 copy.27.z_ref
  194.6 1.3 copy.25.x_ref
  195.9 1.3 copy.26.y_ref
  197.3 1.4 copy.28.slots_ref
  198.6 1.4 copy.29.read_ref
  200.1 34.7 %all-gather.3.cloned.1.call-done = bf16[128,32,256]{2,1,0:T(8,128)(2,1)} async-done(((bf16[4,32,256]{2,1,0:T(8,128)(2,1)}), bf16[128,32,256]{2,1,0:T(8,128)(2,1)}) %all-gather.3.cloned.1.call-update) | async-done | bytes 2097168 | tf_op jit(solution)/shard_map/all_gather | solution.py:295
  234.8 12.9 %inverse.1.inverse_ref = f32[2048,256]{1,0:T(8,128)} custom-call(s32[2048,1]{1,0:T(8,128)} %copy.25.x_ref, s32[2048,1]{1,0:T(8,128)} %copy.26.y_ref, s32[2048,1]{1,0:T(8,128)} %copy.27.z_ref, bf16[128,256]{1,0:T(8,128)(2,1)} %constant.90.clone.tx_ref, bf16[128,16]{1,0:T(8,128)(2,1)} %constant.91.clone.ty_ref, bf16[128,256]{1,0:T(8,128)(2,1)} %constant.92.clone.tz_ref, ...), custom_call_target="tpu_custom_call" | custom-call | flops 4294967296 | bytes 2097152 | tf_op jit(solution)/shard_map/inverse/pallas_call | solution.py:198
  247.7 1.1 copy-done.2
  248.9 12.0 %decode.1 = bf16[2048,256]{1,0:T(8,128)(2,1)} custom-call(s32[2048,1]{1,0:T(8,128)} %copy.28.slots_ref, bf16[3072,256]{1,0:T(8,128)(2,1)} %bitcast.30, f32[2048,256]{1,0:T(8,128)} %inverse.1.inverse_ref, f32[2048,1]{1,0:T(8,128)} %copy.29.read_ref, bf16[256,256]{1,0:T(8,128)(2,1)} %skip_ref.1, bf16[256,256]{1,0:T(8,128)(2,1)} %hidden_ref.1, ...), custom_call_target="tpu_custom_call" | custom-call | flops 3221225472 | bytes 3145728 | tf_op jit(solution)/shard_map/decode/pallas_call | solution.py:232
  (29 shorter events, 3.2 us)
Async XLA Ops:
  6.5 1.4 copy-start
  6.5 158.0 %reduce-scatter.2.cloned.1.call-start = ((), (), s32[]{:S(2)}) async-start(), calls=%async_computation.4 | async-start | bytes 2162688 | tf_op jit(solution)/shard_map/reduce_scatter | solution.py:291
  21.8 0.7 copy-start.3
  52.0 125.8 %all-to-all-start.1 = ((bf16[32,96,256]{2,1,0:T(8,128)(2,1)}), bf16[32,96,256]{2,1,0:T(8,128)(2,1)S(1)}, u32[]{:S(2)}, u32[]{:S(2)}) async-start(bf16[32,96,256]{2,1,0:T(8,128)(2,1)} %bitcast.28), calls=%async_computation.1 | async-start | bytes 3145728 | tf_op jit(solution)/shard_map/all_to_all | solution.py:287
  54.7 180.1 %all-gather.3.cloned.1.call-start = ((), (), s32[]{:S(2)}) async-start(), calls=%async_computation.5 | async-start | bytes 2162688 | tf_op jit(solution)/shard_map/all_gather | solution.py:295
  177.8 1.2 copy-start.1
  190.4 4.2 %copy-start.5 = (s32[2048]{0:T(1024)S(1)}, s32[2048]{0:T(1024)}, u32[]{:S(2)}) copy-start(s32[2048]{0:T(1024)} %get-tuple-element.12) | copy-start | bytes 24580
  190.4 5.6 %copy-start.4 = (s32[2048]{0:T(1024)S(1)}, s32[2048]{0:T(1024)}, u32[]{:S(2)}) copy-start(s32[2048]{0:T(1024)} %get-tuple-element.11) | copy-start | bytes 24580
  190.4 57.4 %all-to-all-start.2 = ((bf16[32,96,256]{2,1,0:T(8,128)(2,1)}), bf16[32,96,256]{2,1,0:T(8,128)(2,1)S(1)}, u32[]{:S(2)}, u32[]{:S(2)}) async-start(bf16[32,96,256]{2,1,0:T(8,128)(2,1)} %bitcast.31), calls=%async_computation.2 | async-start | bytes 3145728 | tf_op jit(solution)/shard_map/all_to_all | solution.py:299
  193.2 4.1 %copy-start.7 = (s32[1,2048]{1,0:T(1,128)S(1)}, s32[1,2048]{1,0:T(1,128)}, u32[]{:S(2)}) copy-start(s32[1,2048]{1,0:T(1,128)} %get-tuple-element.8) | copy-start | bytes 24580
  193.2 5.4 %copy-start.6 = (f32[2048]{0:T(1024)S(1)}, f32[2048]{0:T(1024)}, u32[]{:S(2)}) copy-start(f32[2048]{0:T(1024)} %param.17) | copy-start | bytes 24580
  247.7 1.2 copy-start.2
Sparse Core Ops, SparseCore 0:
  21.9 142.5 reduce-scatter.1
  173.4 61.3 all-gather.2
where the time goes:
time: 268 us
  waiting for transfers between devices  145 us (54%)
  Pallas kernels  59.6 us (22%)
  local copies, waits for them, and re-layouts  15.8 us (6%)
  blocking collectives  14.3 us (5%)
  between operations  13.5 us (5%)
  matrix products  10.4 us (4%)
  starting transfers between devices  5.55 us (2%)
  other arithmetic  4.08 us (2%)
    reduce_scatter x1, waiting for transfers between devices, per_device(): lax.psum_scatter(partial, axes, scatter_dimension=0, tiled=True)[0]  110 us
    all_gather x1, waiting for transfers between devices, per_device(): gathered = lax.all_gather(mixed, axes, axis=0)  34.7 us
    all_to_all x1, blocking collectives, per_device(): lax.all_to_all(send_where.reshape(devices, capacity), axes, split_axis=0,...  14.3 us
    pallas_call x1, Pallas kernels, inverse(): pl.pallas_call(functools.partial(inverse_kernel, modes), grid=(points //...  12.9 us
    pallas_call x1, Pallas kernels, decode(): pl.pallas_call(decode_kernel, grid=(points // block,), in_specs=[column,...  12 us
    pallas_call x1, Pallas kernels, pack(): pl.pallas_call(functools.partial(pack_kernel, devices, capacity), grid=(t...  11.8 us
    pallas_call x1, Pallas kernels, forward(): pl.pallas_call(forward_kernel, grid=(modes,), in_specs=[whole((1, points)...  11.5 us
    pallas_call x1, Pallas kernels, merge(): pl.pallas_call(merge_kernel, grid=(total // block,), in_specs=[pl.BlockSp...  11.4 us
  transfers between devices with their start and end apart: 4, of which 2 were waited for; matrix products, arithmetic and copies ran while one was open for 9% of the time, Pallas kernels for 13%

commit v1 on v0

--- a/solution.py
+++ b/solution.py
@@ -288,12 +288,16 @@
 
     partial = forward(x[None, :], y[None, :], z[None, :], tables, message, axis_first, modes)
     partial = partial.reshape(devices, modes_y, share, width)
-    spectrum = lax.psum_scatter(partial, axes, scatter_dimension=0, tiled=True)[0]
+    partial = partial.reshape(axis_first, axis_second, modes_y, share, width)
+    partial = lax.all_to_all(partial, 'ba', split_axis=1, concat_axis=1, tiled=True)
+    partial = jnp.sum(partial.astype(F32), axis=1).astype(BF16)
+    partial = lax.all_to_all(partial, 'aa', split_axis=0, concat_axis=0, tiled=True)
+    spectrum = jnp.sum(partial.astype(F32), axis=0).astype(BF16)
     mixed = jnp.einsum(
         "jmc,jmco->jmo", spectrum, spectral_weight, preferred_element_type=F32
     ).astype(BF16)
-    gathered = lax.all_gather(mixed, axes, axis=0)
-    gathered = gathered.reshape(axis_first, modes, share, width)
+    gathered = lax.all_gather(mixed, 'ba', axis=0, tiled=True)
+    gathered = lax.all_gather(gathered, 'aa', axis=0)
 
     merged = merge(recv_where, recv_rows)
     returned = lax.all_to_all(merged, axes, split_axis=0, concat_axis=0, tiled=True)

time: 268 us -> 213 us (0.79)
  waiting for transfers between devices: 145 us -> 60.8 us
  blocking collectives: 14.3 us -> 25.9 us
  starting transfers between devices: 5.55 us -> 16.6 us
  local copies, waits for them, and re-layouts: 15.8 us -> 20.1 us
    reduce_scatter x1 -> x0, waiting for transfers between devices: 110 us -> none  [per_device(): lax.psum_scatter(partial, axes, scatter_dimension=0, tiled=True)[0]]
    all_gather x1, waiting for transfers between devices: 34.7 us -> 3.81 us  [per_device(): gathered = lax.all_gather(gathered, 'aa', axis=0)]
    all_to_all x1, waiting for transfers between devices: 0.01 us -> 25.6 us  [per_device(): lax.all_to_all(send_rows, axes, split_axis=0, concat_axis=0, tiled=True)]
    all_to_all x1, waiting for transfers between devices: 0.01 us -> 17.4 us  [per_device(): lax.all_to_all(merged, axes, split_axis=0, concat_axis=0, tiled=True)]
    all_to_all x0 -> x2, waiting for transfers between devices: none -> 14 us  [the longest x1 8.12 us: per_device(): lax.all_to_all(partial, 'ba', split_axis=1, concat_axis=1, tiled=True)]
    all_to_all x0 -> x2, starting transfers between devices: none -> 10.1 us  [the longest x1 5.72 us: per_device(): lax.all_to_all(send_where.reshape(devices, capacity), axes, split_axis=0,...]
    all_gather x0 -> x1, blocking collectives: none -> 7.67 us  [per_device(): gathered = lax.all_gather(mixed, 'ba', axis=0, tiled=True)]
    all_to_all x1, blocking collectives: 14.3 us -> 18.2 us  [per_device(): lax.all_to_all(partial, 'aa', split_axis=0, concat_axis=0, tiled=True)]
  transfers between devices with their start and end apart: 4 -> 5, of which waited for: 2 -> 5; matrix products, arithmetic and copies ran while one was open for 9% -> 12% of each run, Pallas kernels for 13% -> 17%
where the time goes in v1:
time: 213 us; the launch traced here: 212 us
  waiting for transfers between devices  60.8 us (29%)
  Pallas kernels  59.6 us (28%)
  blocking collectives  25.9 us (12%)
  local copies, waits for them, and re-layouts  20.1 us (9%)
  starting transfers between devices  16.6 us (8%)
  between operations  13.5 us (6%)
  matrix products  10.4 us (5%)
  other arithmetic  5.47 us (3%)
    all_to_all x1, waiting for transfers between devices, per_device(): lax.all_to_all(send_rows, axes, split_axis=0, concat_axis=0, tiled=True)  25.6 us
    all_to_all x1, blocking collectives, per_device(): lax.all_to_all(partial, 'aa', split_axis=0, concat_axis=0, tiled=True)  18.2 us
    all_to_all x1, waiting for transfers between devices, per_device(): lax.all_to_all(merged, axes, split_axis=0, concat_axis=0, tiled=True)  17.4 us
    pallas_call x1, Pallas kernels, inverse(): pl.pallas_call(functools.partial(inverse_kernel, modes), grid=(points //...  12.9 us
    pallas_call x1, Pallas kernels, decode(): pl.pallas_call(decode_kernel, grid=(points // block,), in_specs=[column,...  12 us
    pallas_call x1, Pallas kernels, pack(): pl.pallas_call(functools.partial(pack_kernel, devices, capacity), grid=(t...  11.8 us
    pallas_call x1, Pallas kernels, forward(): pl.pallas_call(forward_kernel, grid=(modes,), in_specs=[whole((1, points)...  11.5 us
    pallas_call x1, Pallas kernels, merge(): pl.pallas_call(merge_kernel, grid=(total // block,), in_specs=[pl.BlockSp...  11.4 us
  transfers between devices with their start and end apart: 5, of which 5 were waited for; matrix products, arithmetic and copies ran while one was open for 12% of the time, Pallas kernels for 17%

profile of v1, /device:TPU:0, one launch (start us, length us, event | category | flops | bytes accessed | tf_op | source)
XLA Modules:
  0.0 212.2 jit_solution(13492753506645783550)
XLA Ops:
  6.5 1.4 fusion.7
  8.0 2.3 %fusion.message_ref = bf16[2048,256]{1,0:T(8,128)(2,1)} fusion(bf16[2048,256]{1,0:T(8,128)(2,1)S(1)} %copy-done, bf16[256,256]{1,0:T(8,128)(2,1)} %param.18, f32[2048]{0:T(1024)} %param.16), kind=kOutput, calls=%fused_computation.1 | convolution fusion | flops 269484032 | bytes 2236416 | tf_op jit(solution)/shard_map/dot_general | solution.py:34
  10.3 11.5 %forward.1 = bf16[8,16,32,256]{3,2,1,0:T(8,128)(2,1)} custom-call(s32[1,2048]{1,0:T(1,128)} %bitcast.39, s32[1,2048]{1,0:T(1,128)} %bitcast.37, s32[1,2048]{1,0:T(1,128)} %bitcast.34, bf16[256,128]{1,0:T(8,128)(2,1)} %constant.98.tx_ref, bf16[16,128]{1,0:T(8,128)(2,1)} %constant.99.ty_ref, bf16[256,128]{1,0:T(8,128)(2,1)} %constant.100.tz_ref, ...), custom_call_target="tpu_custom_call" | custom-call | flops 4294967296 | bytes 2097152 | tf_op jit(solution)/shard_map/forward/pallas_call | solution.py:156
  21.8 3.2 %copy.34 = bf16[8,4,4,32,256]{4,3,2,0,1:T(8,128)(2,1)} copy(bf16[8,4,4,32,256]{4,3,2,1,0:T(8,128)(2,1)} %bitcast.26) | data formatting | bytes 4194304 | tf_op jit(solution)/shard_map/reshape;reshape | solution.py:291
  25.0 4.4 %all-to-all-start.3 = ((bf16[8,4,4,32,256]{4,3,2,0,1:T(8,128)(2,1)}), bf16[8,4,4,32,256]{4,3,2,0,1:T(8,128)(2,1)S(1)}, u32[]{:S(2)}, u32[]{:S(2)}) async-start(bf16[8,4,4,32,256]{4,3,2,0,1:T(8,128)(2,1)} %copy.34), calls=%async_computation.3 | async-start | bytes 4194304 | tf_op jit(solution)/shard_map/all_to_all | solution.py:292
  30.6 2.0 pad.4.cells_ref
  32.6 11.8 %pack.1 = (bf16[3072,256]{1,0:T(8,128)(2,1)}, f32[3072,1]{1,0:T(8,128)}, s32[1,2048]{1,0:T(1,128)}) custom-call(s32[1,2048]{1,0:T(1,128)} %bitcast.44, bf16[2048,128]{1,0:T(8,128)(2,1)} %pad.4.cells_ref, bf16[2048,256]{1,0:T(8,128)(2,1)} %fusion.message_ref), custom_call_target="tpu_custom_call" | custom-call | flops 6442450944 | bytes 4718592 | tf_op jit(solution)/shard_map/pack/pallas_call | solution.py:73
  44.4 1.9 reduce.2
  46.9 8.1 %all-to-all-done.3 = bf16[8,4,4,32,256]{4,3,2,0,1:T(8,128)(2,1)S(1)} async-done(((bf16[8,4,4,32,256]{4,3,2,0,1:T(8,128)(2,1)}), bf16[8,4,4,32,256]{4,3,2,0,1:T(8,128)(2,1)S(1)}, u32[]{:S(2)}, u32[]{:S(2)}) %all-to-all-start.3) | async-done | bytes 2097184 | tf_op jit(solution)/shard_map/all_to_all | solution.py:292
  55.0 5.7 %all-to-all-start = ((f32[32,1,96]{2,1,0:T(1,128)}), f32[32,1,96]{2,1,0:T(1,128)S(1)}, u32[]{:S(2)}, u32[]{:S(2)}) async-start(f32[32,1,96]{2,1,0:T(1,128)} %bitcast.3), calls=%async_computation | async-start | bytes 32768 | tf_op jit(solution)/shard_map/all_to_all | solution.py:284
  62.1 5.9 %all-to-all-done = f32[32,1,96]{2,1,0:T(1,128)S(1)} async-done(((f32[32,1,96]{2,1,0:T(1,128)}), f32[32,1,96]{2,1,0:T(1,128)S(1)}, u32[]{:S(2)}, u32[]{:S(2)}) %all-to-all-start) | async-done | bytes 12320 | tf_op jit(solution)/shard_map/all_to_all | solution.py:284
  67.9 18.2 %all_to_all.41 = bf16[8,4,32,256]{3,2,1,0:T(8,128)(2,1)S(1)} all-to-all(bf16[8,4,32,256]{3,2,1,0:T(8,128)(2,1)} %reduce_sum.24), channel_id=1, replica_groups=mesh['aa'=8,'ba'=4] {'aa'}, dimensions={0} | all-to-all | bytes 1048576 | tf_op jit(solution)/shard_map/all_to_all | solution.py:294
  86.1 2.7 %all-to-all-start.1 = ((bf16[32,96,256]{2,1,0:T(8,128)(2,1)}), bf16[32,96,256]{2,1,0:T(8,128)(2,1)S(1)}, u32[]{:S(2)}, u32[]{:S(2)}) async-start(bf16[32,96,256]{2,1,0:T(8,128)(2,1)} %bitcast.27), calls=%async_computation.1 | async-start | bytes 3145728 | tf_op jit(solution)/shard_map/all_to_all | solution.py:287
  89.0 8.0 %fusion.1 = bf16[4,32,1,256]{3,2,1,0:T(2,128)(2,1)S(1)} fusion(bf16[4,32,256,256]{3,2,1,0:T(8,128)(2,1)} %param.20, bf16[4,32,256,1]{2,1,0,3:T(8,128)(2,1)S(1)} %bitcast.31), kind=kOutput, calls=%fused_computation.3 | convolution fusion | flops 16777216 | bytes 16908288 | tf_op jit(solution)/shard_map/jmc,jmco->jmo/dot_general | solution.py:296
  97.1 7.7 %all_gather.9 = bf16[16,32,256]{2,1,0:T(8,128)(2,1)} all-gather(bf16[4,32,256]{2,1,0:T(8,128)(2,1)S(1)} %bitcast.32), channel_id=1, replica_groups=mesh['aa'=8,'ba'=4] {'ba'}, dimensions={0}, use_global_device_ids=true | all-gather | bytes 327680 | tf_op jit(solution)/shard_map/all_gather | solution.py:299
  106.0 2.7 %reshape.26.column_ref = f32[3072,1]{1,0:T(8,128)} reshape(f32[32,96]{1,0:T(8,128)S(1)} %reduce.8) | data formatting | bytes 24576 | tf_op jit(solution)/shard_map/reshape | solution.py:121
  109.3 25.6 %all-to-all-done.1 = bf16[32,96,256]{2,1,0:T(8,128)(2,1)S(1)} async-done(((bf16[32,96,256]{2,1,0:T(8,128)(2,1)}), bf16[32,96,256]{2,1,0:T(8,128)(2,1)S(1)}, u32[]{:S(2)}, u32[]{:S(2)}) %all-to-all-start.1) | async-done | bytes 1572896 | tf_op jit(solution)/shard_map/all_to_all | solution.py:287
  136.1 11.4 %merge.1 = bf16[3072,256]{1,0:T(8,128)(2,1)} custom-call(f32[3072,1]{1,0:T(8,128)} %reshape.26.column_ref, f32[1,3072]{1,0:T(1,128)} %reshape.22.row_ref, bf16[3072,256]{1,0:T(8,128)(2,1)} %bitcast.28), custom_call_target="tpu_custom_call" | custom-call | flops 4831838208 | bytes 3145728 | tf_op jit(solution)/shard_map/merge/pallas_call | solution.py:107
  147.5 3.8 %all-to-all-start.2 = ((bf16[32,96,256]{2,1,0:T(8,128)(2,1)}), bf16[32,96,256]{2,1,0:T(8,128)(2,1)S(1)}, u32[]{:S(2)}, u32[]{:S(2)}) async-start(bf16[32,96,256]{2,1,0:T(8,128)(2,1)} %bitcast.30), calls=%async_computation.2 | async-start | bytes 3145728 | tf_op jit(solution)/shard_map/all_to_all | solution.py:303
  156.7 1.5 copy.39.read_ref
  158.2 3.8 %all-gather.3.cloned.1.call-done = bf16[128,32,256]{2,1,0:T(8,128)(2,1)} async-done(((bf16[16,32,256]{2,1,0:T(8,128)(2,1)}), bf16[128,32,256]{2,1,0:T(8,128)(2,1)}) %all-gather.3.cloned.1.call-update) | async-done | bytes 2097168 | tf_op jit(solution)/shard_map/all_gather | solution.py:300
  162.0 12.9 %inverse.1.inverse_ref = f32[2048,256]{1,0:T(8,128)} custom-call(s32[2048,1]{1,0:T(8,128)} %copy.35.x_ref, s32[2048,1]{1,0:T(8,128)} %copy.36.y_ref, s32[2048,1]{1,0:T(8,128)} %copy.37.z_ref, bf16[128,256]{1,0:T(8,128)(2,1)} %constant.93.clone.tx_ref, bf16[128,16]{1,0:T(8,128)(2,1)} %constant.94.clone.ty_ref, bf16[128,256]{1,0:T(8,128)(2,1)} %constant.95.clone.tz_ref, ...), custom_call_target="tpu_custom_call" | custom-call | flops 4294967296 | bytes 2097152 | tf_op jit(solution)/shard_map/inverse/pallas_call | solution.py:198
  174.9 17.4 %all-to-all-done.2 = bf16[32,96,256]{2,1,0:T(8,128)(2,1)S(1)} async-done(((bf16[32,96,256]{2,1,0:T(8,128)(2,1)}), bf16[32,96,256]{2,1,0:T(8,128)(2,1)S(1)}, u32[]{:S(2)}, u32[]{:S(2)}) %all-to-all-start.2) | async-done | bytes 1572896 | tf_op jit(solution)/shard_map/all_to_all | solution.py:303
  193.4 12.0 %decode.1 = bf16[2048,256]{1,0:T(8,128)(2,1)} custom-call(s32[2048,1]{1,0:T(8,128)} %copy.38.slots_ref, bf16[3072,256]{1,0:T(8,128)(2,1)} %bitcast.29, f32[2048,256]{1,0:T(8,128)} %inverse.1.inverse_ref, f32[2048,1]{1,0:T(8,128)} %copy.39.read_ref, bf16[256,256]{1,0:T(8,128)(2,1)} %skip_ref.1, bf16[256,256]{1,0:T(8,128)(2,1)} %hidden_ref.1, ...), custom_call_target="tpu_custom_call" | custom-call | flops 3221225472 | bytes 3145728 | tf_op jit(solution)/shard_map/decode/pallas_call | solution.py:232
  (34 shorter events, 13.0 us)
Async XLA Ops:
  6.5 1.4 copy-start
  25.0 4.4 %copy-start.3 = (s32[2048]{0:T(1024)S(1)}, s32[2048]{0:T(1024)}, u32[]{:S(2)}) copy-start(s32[2048]{0:T(1024)} %get-tuple-element.13) | copy-start | bytes 24580
  25.0 30.1 %all-to-all-start.3 = ((bf16[8,4,4,32,256]{4,3,2,0,1:T(8,128)(2,1)}), bf16[8,4,4,32,256]{4,3,2,0,1:T(8,128)(2,1)S(1)}, u32[]{:S(2)}, u32[]{:S(2)}) async-start(bf16[8,4,4,32,256]{4,3,2,0,1:T(8,128)(2,1)} %copy.34), calls=%async_computation.3 | async-start | bytes 4194304 | tf_op jit(solution)/shard_map/all_to_all | solution.py:292
  55.0 12.9 %all-to-all-start = ((f32[32,1,96]{2,1,0:T(1,128)}), f32[32,1,96]{2,1,0:T(1,128)S(1)}, u32[]{:S(2)}, u32[]{:S(2)}) async-start(f32[32,1,96]{2,1,0:T(1,128)} %bitcast.3), calls=%async_computation | async-start | bytes 32768 | tf_op jit(solution)/shard_map/all_to_all | solution.py:284
  86.1 48.8 %all-to-all-start.1 = ((bf16[32,96,256]{2,1,0:T(8,128)(2,1)}), bf16[32,96,256]{2,1,0:T(8,128)(2,1)S(1)}, u32[]{:S(2)}, u32[]{:S(2)}) async-start(bf16[32,96,256]{2,1,0:T(8,128)(2,1)} %bitcast.27), calls=%async_computation.1 | async-start | bytes 3145728 | tf_op jit(solution)/shard_map/all_to_all | solution.py:287
  88.9 73.1 %all-gather.3.cloned.1.call-start = ((), (), s32[]{:S(2)}) async-start(), calls=%async_computation.5 | async-start | bytes 2359296 | tf_op jit(solution)/shard_map/all_gather | solution.py:300
  134.9 1.2 copy-start.1
  147.5 5.2 %copy-start.5 = (s32[2048]{0:T(1024)S(1)}, s32[2048]{0:T(1024)}, u32[]{:S(2)}) copy-start(s32[2048]{0:T(1024)} %get-tuple-element.12) | copy-start | bytes 24580
  147.5 6.5 %copy-start.4 = (s32[2048]{0:T(1024)S(1)}, s32[2048]{0:T(1024)}, u32[]{:S(2)}) copy-start(s32[2048]{0:T(1024)} %get-tuple-element.11) | copy-start | bytes 24580
  147.5 44.8 %all-to-all-start.2 = ((bf16[32,96,256]{2,1,0:T(8,128)(2,1)}), bf16[32,96,256]{2,1,0:T(8,128)(2,1)S(1)}, u32[]{:S(2)}, u32[]{:S(2)}) async-start(bf16[32,96,256]{2,1,0:T(8,128)(2,1)} %bitcast.30), calls=%async_computation.2 | async-start | bytes 3145728 | tf_op jit(solution)/shard_map/all_to_all | solution.py:303
  151.3 4.1 %copy-start.7 = (s32[1,2048]{1,0:T(1,128)S(1)}, s32[1,2048]{1,0:T(1,128)}, u32[]{:S(2)}) copy-start(s32[1,2048]{1,0:T(1,128)} %get-tuple-element.8) | copy-start | bytes 24580
  151.3 5.4 %copy-start.6 = (f32[2048]{0:T(1024)S(1)}, f32[2048]{0:T(1024)}, u32[]{:S(2)}) copy-start(f32[2048]{0:T(1024)} %param.17) | copy-start | bytes 24580
  192.3 1.1 copy-start.2
Sparse Core Ops, SparseCore 0:
  104.9 57.0 all-gather.2
